TPU v7x, 32 devices: a whole 2x2x4 slice. The times are simulated.
32 devices in a mesh: lat: 8 (over z, y), ch: 4 (over x, core).
Axes of the slice: x: 2, y: 2, z: 4, core: 2. Of those that a mesh axis runs over, the one named last changes fastest.
Arguments:
- field_in: bfloat16 [768, 384, 768], P('ch', 'lat'), may hold values from -80 to 80
- ln_gain: float32 [2, 768], P(None, 'ch'), may hold values from 0.5 to 1.5
- ln_shift: float32 [2, 768], P(None, 'ch'), may hold values from -1.5 to 1.5
- mix_first: bfloat16 [2, 2, 8, 96, 96], P(None, None, 'ch'), may hold values from -0.4375 to 0.4375
- mix_bias: bfloat16 [2, 2, 8, 96], P(None, None, 'ch'), may hold values from -3 to 3
- mix_second: bfloat16 [2, 2, 8, 96, 96], P(None, None, 'ch'), may hold values from -0.4375 to 0.4375
Outputs:
- field_out: bfloat16 [768, 384, 768], P('ch', 'lat')
All inputs are finite; a program needn't handle non-finite values.
Results may differ from a plain program's by a relative error of at most 0.014.
Values may be sent and summed in bfloat16 or wider, within the bound.
A program may use at most 256 MiB of HBM per device.

v0:
```python
import math

import jax
import jax.numpy as jnp
from jax import lax
from jax.sharding import PartitionSpec as P

norm_eps = 1e-05
shrink_level = 0.01


def soft_shrink(values):
    return jnp.sign(values) * jnp.maximum(jnp.abs(values) - shrink_level, 0.0)


def trig_angles(length, freq_ids):
    positions = jnp.arange(length, dtype=jnp.int32)
    phase_ids = positions[:, None] * freq_ids[None, :] % length
    angles = phase_ids.astype(jnp.float32) * (2.0 * math.pi / length)
    norm_scale = 1.0 / math.sqrt(length)
    return (jnp.cos(angles) * norm_scale, jnp.sin(angles) * norm_scale)


def lon_tables(lon_cells, pieces):
    mode_count = lon_cells // 2
    per_piece = mode_count // pieces
    column = jnp.arange(2 * mode_count, dtype=jnp.int32)
    is_imag = column // per_piece % 2
    freq_ids = column // (2 * per_piece) * per_piece + column % per_piece
    cos_part, sin_part = trig_angles(lon_cells, freq_ids)
    forward = jnp.where(is_imag[None, :] == 0, cos_part, -sin_part).astype(jnp.bfloat16)
    weight_k = jnp.where(freq_ids == 0, 1.0, 2.0).astype(jnp.float32)
    inverse = (forward.astype(jnp.float32).T * weight_k[:, None]).astype(jnp.bfloat16)
    return (forward, inverse)


def normalize(source, gain, shift):
    ch_all = source.shape[0] * lax.axis_size("ch")
    total_sum, squares = (
        lax.psum(jnp.sum(source, axis=0).astype(jnp.bfloat16), "ch").astype(jnp.float32),
        lax.psum(jnp.sum(source * source, axis=0).astype(jnp.bfloat16), "ch").astype(jnp.float32),
    )
    mean_val = total_sum / ch_all
    spread = squares / ch_all - mean_val * mean_val
    inv_std = lax.rsqrt(spread + norm_eps)
    gain_col = gain[:, None, None]
    shift_col = shift[:, None, None]
    return ((source - mean_val) * inv_std * gain_col + shift_col).astype(jnp.bfloat16)


def lat_transform(mode_data, cos_lat, sin_lat, backward):
    chans, lat_rows, width_q = mode_data.shape
    part_cos = jnp.einsum("hj,chq->cjq", cos_lat, mode_data, preferred_element_type=jnp.float32)
    part_sin = jnp.einsum("hj,chq->cjq", sin_lat, mode_data, preferred_element_type=jnp.float32)
    part_cos = part_cos.reshape(chans, lat_rows, 2, width_q // 2)
    part_sin = part_sin.reshape(chans, lat_rows, 2, width_q // 2)
    if backward:
        real_part = part_cos[:, :, 0] - part_sin[:, :, 1]
        imag_part = part_cos[:, :, 1] + part_sin[:, :, 0]
    else:
        real_part = part_cos[:, :, 0] + part_sin[:, :, 1]
        imag_part = part_cos[:, :, 1] - part_sin[:, :, 0]
    return jnp.stack([real_part, imag_part], axis=2).astype(jnp.bfloat16)


def contract(operand, weight):
    return jnp.einsum("bcjm,bcd->bdjm", operand, weight, preferred_element_type=jnp.float32)


def block_mix(lat_spec, first_w, first_b, second_w, block_width):
    chans, lat_rows, two_parts, per_piece = lat_spec.shape
    block_count = chans // block_width
    grouped = lat_spec.reshape(block_count, block_width, lat_rows, two_parts, per_piece)
    spec_re = grouped[:, :, :, 0]
    spec_im = grouped[:, :, :, 1]
    bias_f = first_b.astype(jnp.float32)
    hid_re = jax.nn.relu(
        contract(spec_re, first_w[0]) - contract(spec_im, first_w[1]) + bias_f[0][:, :, None, None]
    ).astype(jnp.bfloat16)
    hid_im = jax.nn.relu(
        contract(spec_im, first_w[0]) + contract(spec_re, first_w[1]) + bias_f[1][:, :, None, None]
    ).astype(jnp.bfloat16)
    mix_re = soft_shrink(contract(hid_re, second_w[0]) - contract(hid_im, second_w[1])).astype(
        jnp.bfloat16
    )
    mix_im = soft_shrink(contract(hid_im, second_w[0]) + contract(hid_re, second_w[1])).astype(
        jnp.bfloat16
    )
    return jnp.stack([mix_re, mix_im], axis=3).reshape(chans, lat_rows, two_parts * per_piece)


def per_device(field_in, ln_gain, ln_shift, mix_first, mix_bias, mix_second):
    lat_parts = lax.axis_size("lat")
    ch_dev, band_rows, lon_cells = field_in.shape
    lat_rows = band_rows * lat_parts
    block_width = mix_first.shape[-1]
    first_all, bias_all, second_all = (mix_first, mix_bias, mix_second)
    per_piece = lon_cells // 2 // lat_parts
    forward, inverse = lon_tables(lon_cells, lat_parts)
    cos_f, sin_f = trig_angles(lat_rows, jnp.arange(lat_rows, dtype=jnp.int32))
    cos_lat = cos_f.astype(jnp.bfloat16)
    sin_lat = sin_f.astype(jnp.bfloat16)
    row_pos = (lax.axis_index("lat") * band_rows + jnp.arange(band_rows, dtype=jnp.int32)).astype(
        jnp.float32
    )
    area_weights = jnp.cos((row_pos + 0.5) * (math.pi / lat_rows) - 0.5 * math.pi)[None, :, None]
    source = field_in.astype(jnp.float32)
    target = lax.psum(jnp.sum(area_weights * source * source), ("lat", "ch"))
    current = field_in
    for layer_idx in range(mix_first.shape[0]):
        normed = normalize(source, ln_gain[layer_idx], ln_shift[layer_idx])
        lon_spec = jnp.dot(
            normed.reshape(ch_dev * band_rows, lon_cells),
            forward,
            preferred_element_type=jnp.float32,
        ).astype(jnp.bfloat16)
        mode_data = lax.all_to_all(
            lon_spec.reshape(ch_dev, band_rows, lon_cells),
            "lat",
            split_axis=2,
            concat_axis=1,
            tiled=True,
        )
        lat_spec = lat_transform(mode_data, cos_lat, sin_lat, False)
        mixed_spec = block_mix(
            lat_spec, first_all[layer_idx], bias_all[layer_idx], second_all[layer_idx], block_width
        )
        back_spec = lat_transform(mixed_spec, cos_lat, sin_lat, True).reshape(
            ch_dev, lat_rows, 2 * per_piece
        )
        band_spec = lax.all_to_all(back_spec, "lat", split_axis=1, concat_axis=2, tiled=True)
        spatial = jnp.dot(
            band_spec.reshape(ch_dev * band_rows, lon_cells),
            inverse,
            preferred_element_type=jnp.float32,
        )
        spatial = spatial.reshape(ch_dev, band_rows, lon_cells)
        summed = spatial + normed.astype(jnp.float32) + current.astype(jnp.float32)
        energy = lax.psum(jnp.sum(area_weights * summed * summed), ("lat", "ch"))
        current = (summed * jnp.sqrt(target / energy)).astype(jnp.bfloat16)
        source = summed
    return current


def solution(mesh):
    return jax.shard_map(
        per_device,
        mesh=mesh,
        in_specs=(
            P("ch", "lat", None),
            P(None, "ch"),
            P(None, "ch"),
            P(None, None, "ch", None, None),
            P(None, None, "ch", None),
            P(None, None, "ch", None, None),
        ),
        out_specs=P("ch", "lat", None),
        check_vma=False,
    )
```

profile of v0, /device:TPU:0, one launch (start us, length us, event | category | flops | bytes accessed | tf_op | source)
XLA Modules:
  0.0 2720.7 jit_solution(8269819669028374441)
XLA Ops:
  6.6 13.2 fusion.7
  38.8 22.7 all-reduce.8.cloned.1.call-done
  62.5 15.9 fusion.5
  78.4 19.0 convolution_convert_fusion.1
  97.4 26.2 copy.105
  130.5 407.0 %all-to-all-done = bf16[192,48,768]{0,1,2:T(8,128)(2,1)} async-done(((bf16[192,48,768]{0,1,2:T(8,128)(2,1)}), bf16[192,48,768]{0,1,2:T(8,128)(2,1)}, u32[]{:S(2)}, u32[]{:S(2)}) %all-to-all-start) | async-done | bytes 14155808 | tf_op jit(solution)/shard_map/all_to_all | solution.py:117
  537.5 36.1 %copy.107 = bf16[192,8,48,96]{3,2,1,0:T(8,128)(2,1)} copy(bf16[192,8,48,96]{0,2,3,1:T(8,128)(2,1)} %bitcast.6) | data formatting | bytes 28311552 | tf_op jit(solution)/shard_map/all_to_all | solution.py:117
  573.6 20.4 fusion.76
  594.0 20.7 fusion.84
  614.7 21.7 fusion.15
  650.8 14.3 fusion.17
  675.5 14.5 fusion.16
  700.3 17.0 fusion.21
  717.3 12.2 fusion.20
  737.0 12.5 copy.118
  749.5 20.1 fusion.74
  769.6 20.2 fusion.82
  789.9 18.4 fusion.13
  814.5 22.6 copy.119
  843.8 11.1 fusion.60.clone.4
  854.9 394.9 %all-to-all-done.1 = bf16[192,384,96]{2,0,1:T(8,128)(2,1)} async-done(((bf16[192,384,96]{2,0,1:T(8,128)(2,1)}), bf16[192,384,96]{2,0,1:T(8,128)(2,1)}, u32[]{:S(2)}, u32[]{:S(2)}) %all-to-all-start.1) | async-done | bytes 14155808 | tf_op jit(solution)/shard_map/all_to_all | solution.py:131
  1249.8 20.8 copy.121
  1270.6 29.6 %dot_general.101 = bf16[192,48,768]{2,1,0:T(8,128)(2,1)} reshape(bf16[192,48,8,96]{3,2,1,0:T(8,128)(2,1)} %copy.121) | data formatting | bytes 28311552 | tf_op jit(solution)/shard_map/dot_general | solution.py:132
  1300.3 29.7 %fusion.183 = (bf16[48,768]{1,0:T(8,128)(2,1)}, f32[]{:T(128)}, bf16[48,768]{1,0:T(8,128)(2,1)}, f32[192,48,768]{2,1,0:T(8,128)}) fusion(f32[48]{0:T(128)S(1)} %copy-done.31, f32[192]{0:T(256)S(1)} %bitcast.273, f32[192]{0:T(256)S(1)} %bitcast.275, f32[48,768]{1,0:T(8,128)S(1)} %copy-done.7, f32[48,768]{1,0:T(8,128)S(1)} %copy-done.5, ...), kind=kOutput, calls=%fused_computation.232 | convolution fusion | flops 10977730560 | bytes 58246852 | tf_op jit(solution)/shard_map/dot_general | solution.py:132
  1340.2 19.7 all-reduce.6.cloned.1.call-done
  1360.9 17.8 add_convert_fusion
  1378.8 19.0 convolution_convert_fusion
  1397.7 26.2 copy.122
  1424.0 416.0 %all_to_all.66 = bf16[192,48,768]{0,1,2:T(8,128)(2,1)} all-to-all(bf16[192,48,768]{0,1,2:T(8,128)(2,1)} %copy.122), channel_id=1, replica_groups=mesh['lat'=8,'ch'=4] {'lat'}, dimensions={2} | all-to-all | bytes 28311552 | tf_op jit(solution)/shard_map/all_to_all | solution.py:117
  1840.0 36.1 %copy.124 = bf16[192,8,48,96]{3,2,1,0:T(8,128)(2,1)} copy(bf16[192,8,48,96]{0,2,3,1:T(8,128)(2,1)} %bitcast.249) | data formatting | bytes 28311552 | tf_op jit(solution)/shard_map/all_to_all | solution.py:117
  1876.1 20.2 fusion.72
  1896.4 20.5 fusion.80
  1916.9 21.8 fusion.11
  1953.0 14.3 fusion.19
  1977.6 14.7 fusion.18
  2002.5 17.1 fusion.23
  2019.6 12.0 fusion.22
  2039.1 12.5 copy.135
  2051.6 20.1 fusion.70
  2071.7 20.2 fusion.78
  2091.9 18.4 fusion.9
  2116.6 22.6 copy.136
  2156.1 416.0 %all-reduce = (f32[]{:T(128)}, f32[]{:T(128)}) all-reduce(f32[]{:T(128)} %get-tuple-element.8, f32[]{:T(128)} %get-tuple-element.6), channel_id=1, replica_groups=mesh['lat'=8,'ch'=4] {'lat','ch'}, use_global_device_ids=true, to_apply=%region_9.10 | all-reduce | flops 2 | bytes 16 | tf_op jit(solution)/shard_map/psum | solution.py:108
  2573.4 20.8 copy.138
  2594.2 29.6 %dot_general.116 = bf16[192,48,768]{2,1,0:T(8,128)(2,1)} reshape(bf16[192,48,8,96]{3,2,1,0:T(8,128)(2,1)} %copy.138) | data formatting | bytes 28311552 | tf_op jit(solution)/shard_map/dot_general | solution.py:132
  2623.8 32.9 %fusion.1 = (f32[]{:T(128)}, f32[192,48,768]{2,1,0:T(8,128)}) fusion(f32[48]{0:T(128)S(1)} %copy-done.32, f32[192,48,768]{2,1,0:T(8,128)} %get-tuple-element.38, f32[]{:T(128)S(6)} %sqrt.6, f32[192]{0:T(256)S(1)} %bitcast.269, f32[192]{0:T(256)S(1)} %bitcast.271, f32[48,768]{1,0:T(8,128)S(1)} %copy-done.11, f32[48,768]{1,0:T(8,128)S(1)} %copy-done.9, ...), kind=kOutput, calls=%fused_computation.8 | convolution fusion | flops 10970726400 | bytes 72255176 | tf_op jit(solution)/shard_map/dot_general | solution.py:132
  2656.8 39.2 %psum.55 = f32[]{:T(128)} all-reduce(f32[]{:T(128)} %get-tuple-element.39), channel_id=1, replica_groups=mesh['lat'=8,'ch'=4] {'lat','ch'}, use_global_device_ids=true, to_apply=%region_13.14 | all-reduce | flops 1 | bytes 8 | tf_op jit(solution)/shard_map/psum | solution.py:139
  2697.3 16.1 multiply_convert_fusion
  (116 shorter events, 159.0 us)
Async XLA Ops:
  6.5 55.0 %all-reduce.8.cloned.1.call-start = ((), (), s32[]{:S(2)}) async-start(), calls=%async_computation.5 | async-start | bytes 294912 | tf_op jit(solution)/shard_map/psum | solution.py:41
  6.6 20.9 copy-start.30
  6.6 21.0 copy-start.28
  6.6 31.7 %copy-start.29 = (f32[2,192]{1,0:T(2,128)S(1)}, f32[2,192]{1,0:T(2,128)}, u32[]{:S(2)}) copy-start(f32[2,192]{1,0:T(2,128)} %param.7) | copy-start | bytes 4612
  27.5 0.6 copy-start.22
  27.6 10.7 copy-start.33
  28.1 50.3 %copy-start.18 = (f32[1,192]{1,0:T(1,128)}, f32[1,192]{1,0:T(1,128)S(1)}, u32[]{:S(2)}) copy-start(f32[1,192]{1,0:T(1,128)S(1)} %get-tuple-element.35) | copy-start | bytes 2308
  38.8 39.6 %copy-start.20 = (f32[1,192]{1,0:T(1,128)}, f32[1,192]{1,0:T(1,128)S(1)}, u32[]{:S(2)}) copy-start(f32[1,192]{1,0:T(1,128)S(1)} %get-tuple-element.33) | copy-start | bytes 2308
  62.5 15.9 copy-start.4
  62.5 15.9 copy-start.6
  123.6 6.3 copy-start.27
  123.6 413.9 %all-to-all-start = ((bf16[192,48,768]{0,1,2:T(8,128)(2,1)}), bf16[192,48,768]{0,1,2:T(8,128)(2,1)}, u32[]{:S(2)}, u32[]{:S(2)}) async-start(bf16[192,48,768]{0,1,2:T(8,128)(2,1)} %copy.105), calls=%async_computation | async-start | bytes 37748736 | tf_op jit(solution)/shard_map/all_to_all | solution.py:117
  614.7 21.7 copy-start
  650.8 14.3 copy-start.2
  690.0 27.3 %slice-start.2 = ((s8[7077888]{0:T(1024)(128)(4,1)}), s8[4194304]{0:T(1024)(128)(4,1)S(1)}, s32[]{:S(2)}) async-start(s8[7077888]{0:T(1024)(128)(4,1)} %bitcast.260), calls=%async_computation.8 | async-start | bytes 8388608
  700.3 17.0 slice-start.3
  837.1 6.7 copy-start.23
  837.1 6.7 copy-start.34
  837.1 412.7 %all-to-all-start.1 = ((bf16[192,384,96]{2,0,1:T(8,128)(2,1)}), bf16[192,384,96]{2,0,1:T(8,128)(2,1)}, u32[]{:S(2)}, u32[]{:S(2)}) async-start(bf16[192,384,96]{2,0,1:T(8,128)(2,1)} %copy.119), calls=%async_computation.1 | async-start | bytes 37748736 | tf_op jit(solution)/shard_map/all_to_all | solution.py:131
  843.1 516.8 %all-reduce.6.cloned.1.call-start = ((), (), s32[]{:S(2)}) async-start(), calls=%async_computation.4 | async-start | bytes 294912 | tf_op jit(solution)/shard_map/psum | solution.py:41
  843.2 0.6 copy-start.25
  1270.6 29.6 %copy-start.5 = (f32[48,768]{1,0:T(8,128)S(1)}, f32[48,768]{1,0:T(8,128)}, u32[]{:S(2)}) copy-start(f32[48,768]{1,0:T(8,128)} %copy-done.4) | copy-start | bytes 442372
  1270.6 29.6 %copy-start.7 = (f32[48,768]{1,0:T(8,128)S(1)}, f32[48,768]{1,0:T(8,128)}, u32[]{:S(2)}) copy-start(f32[48,768]{1,0:T(8,128)} %copy-done.6) | copy-start | bytes 442372
  1270.6 29.6 %copy-start.19 = (f32[1,192]{1,0:T(1,128)S(1)}, f32[1,192]{1,0:T(1,128)}, u32[]{:S(2)}) copy-start(f32[1,192]{1,0:T(1,128)} %copy-done.18) | copy-start | bytes 2308
  1270.6 29.6 %copy-start.21 = (f32[1,192]{1,0:T(1,128)S(1)}, f32[1,192]{1,0:T(1,128)}, u32[]{:S(2)}) copy-start(f32[1,192]{1,0:T(1,128)} %copy-done.20) | copy-start | bytes 2308
  1270.6 29.6 %copy-start.31 = (f32[48]{0:T(128)S(1)}, f32[48]{0:T(128)}, u32[]{:S(2)}) copy-start(f32[48]{0:T(128)} %copy-done.30) | copy-start | bytes 580
  1300.2 60.7 %copy-start.14 = (f32[1,192]{1,0:T(1,128)S(1)}, f32[1,192]{1,0:T(1,128)}, u32[]{:S(2)}) copy-start(f32[1,192]{1,0:T(1,128)} %get-tuple-element.34) | copy-start | bytes 2308
  1300.2 60.7 %copy-start.16 = (f32[1,192]{1,0:T(1,128)S(1)}, f32[1,192]{1,0:T(1,128)}, u32[]{:S(2)}) copy-start(f32[1,192]{1,0:T(1,128)} %get-tuple-element.32) | copy-start | bytes 2308
  1360.9 17.9 copy-start.8
  1360.9 17.9 copy-start.10
  1916.9 21.8 copy-start.1
  1946.0 7.0 copy-start.13
  1953.0 14.3 copy-start.3
  1967.3 10.3 copy-start.12
  1992.3 27.3 %slice-start = ((s8[7077888]{0:T(1024)(128)(4,1)}), s8[4194304]{0:T(1024)(128)(4,1)S(1)}, s32[]{:S(2)}) async-start(s8[7077888]{0:T(1024)(128)(4,1)} %bitcast.258), calls=%async_computation.6 | async-start | bytes 8388608
  2002.5 17.1 slice-start.1
  2139.2 6.0 copy-start.24
  2139.2 6.0 copy-start.26
  2139.2 6.0 copy-start.35
  2139.2 434.3 %all-to-all-start.3 = ((bf16[192,384,96]{2,0,1:T(8,128)(2,1)}), bf16[192,384,96]{2,0,1:T(8,128)(2,1)}, u32[]{:S(2)}, u32[]{:S(2)}) async-start(bf16[192,384,96]{2,0,1:T(8,128)(2,1)} %copy.136), calls=%async_computation.3 | async-start | bytes 37748736 | tf_op jit(solution)/shard_map/all_to_all | solution.py:131
  2594.2 29.6 %copy-start.9 = (f32[48,768]{1,0:T(8,128)S(1)}, f32[48,768]{1,0:T(8,128)}, u32[]{:S(2)}) copy-start(f32[48,768]{1,0:T(8,128)} %copy-done.8) | copy-start | bytes 442372
  2594.2 29.6 %copy-start.11 = (f32[48,768]{1,0:T(8,128)S(1)}, f32[48,768]{1,0:T(8,128)}, u32[]{:S(2)}) copy-start(f32[48,768]{1,0:T(8,128)} %copy-done.10) | copy-start | bytes 442372
  2594.2 29.6 %copy-start.15 = (f32[1,192]{1,0:T(1,128)S(1)}, f32[1,192]{1,0:T(1,128)}, u32[]{:S(2)}) copy-start(f32[1,192]{1,0:T(1,128)} %get-tuple-element.34) | copy-start | bytes 2308
  2594.2 29.6 %copy-start.17 = (f32[1,192]{1,0:T(1,128)S(1)}, f32[1,192]{1,0:T(1,128)}, u32[]{:S(2)}) copy-start(f32[1,192]{1,0:T(1,128)} %get-tuple-element.32) | copy-start | bytes 2308
  2594.2 29.6 %copy-start.32 = (f32[48]{0:T(128)S(1)}, f32[48]{0:T(128)}, u32[]{:S(2)}) copy-start(f32[48]{0:T(128)} %copy-done.30) | copy-start | bytes 580
Sparse Core Ops, SparseCore 0:
  27.6 33.8 all-reduce.7
  1330.1 29.7 all-reduce.5
where the time goes:
time: 2740 us; the launch traced here: 2720 us
  blocking collectives  871 us (32%)
  waiting for transfers between devices  844 us (31%)
  matrix products  449 us (16%)
  local copies, waits for them, and re-layouts  298 us (11%)
  other arithmetic  223 us (8%)
    psum x1, blocking collectives, per_device(): target = lax.psum(jnp.sum(area_weights * source * source), ('lat', 'ch'))  416 us
    all_to_all x1, blocking collectives, per_device(): lax.all_to_all(lon_spec.reshape(ch_dev, band_rows, lon_cells), 'lat', spl...  416 us
    all_to_all x1, waiting for transfers between devices, per_device(): lax.all_to_all(lon_spec.reshape(ch_dev, band_rows, lon_cells), 'lat', spl...  407 us
    all_to_all x2, waiting for transfers between devices, per_device(): lax.all_to_all(back_spec, 'lat', split_axis=1, concat_axis=2, tiled=True)  395 us
    dot_general x16, matrix products, contract(): jnp.einsum('bcjm,bcd->bdjm', operand, weight, preferred_element_type=jnp....  186 us
    dot_general x4, matrix products, lat_transform(): jnp.einsum('hj,chq->cjq', cos_lat, mode_data, preferred_element_type=jnp....  81.6 us
    dot_general x4, matrix products, lat_transform(): jnp.einsum('hj,chq->cjq', sin_lat, mode_data, preferred_element_type=jnp....  80.8 us
    another operation x4, other arithmetic  80.3 us
  transfers between devices with their start and end apart: 5, of which 4 were waited for; matrix products, arithmetic and copies ran while one was open for 2% of the time, Pallas kernels for 0%

commit v1 on v0

--- a/solution.py
+++ b/solution.py
@@ -89,6 +89,13 @@
     return jnp.stack([mix_re, mix_im], axis=3).reshape(chans, lat_rows, two_parts * per_piece)
 
 
+def exchange(pieces):
+    parts, chans, rows, width_q = pieces.shape
+    flat = lax.optimization_barrier(pieces.reshape(parts, chans, rows * width_q))
+    flat = lax.all_to_all(flat, "lat", split_axis=0, concat_axis=0, tiled=True)
+    return lax.optimization_barrier(flat).reshape(parts, chans, rows, width_q)
+
+
 def per_device(field_in, ln_gain, ln_shift, mix_first, mix_bias, mix_second):
     lat_parts = lax.axis_size("lat")
     ch_dev, band_rows, lon_cells = field_in.shape
@@ -96,6 +103,7 @@
     block_width = mix_first.shape[-1]
     first_all, bias_all, second_all = (mix_first, mix_bias, mix_second)
     per_piece = lon_cells // 2 // lat_parts
+    block_count = ch_dev // block_width
     forward, inverse = lon_tables(lon_cells, lat_parts)
     cos_f, sin_f = trig_angles(lat_rows, jnp.arange(lat_rows, dtype=jnp.int32))
     cos_lat = cos_f.astype(jnp.bfloat16)
@@ -109,33 +117,48 @@
     current = field_in
     for layer_idx in range(mix_first.shape[0]):
         normed = normalize(source, ln_gain[layer_idx], ln_shift[layer_idx])
-        lon_spec = jnp.dot(
-            normed.reshape(ch_dev * band_rows, lon_cells),
-            forward,
-            preferred_element_type=jnp.float32,
-        ).astype(jnp.bfloat16)
-        mode_data = lax.all_to_all(
-            lon_spec.reshape(ch_dev, band_rows, lon_cells),
-            "lat",
-            split_axis=2,
-            concat_axis=1,
-            tiled=True,
-        )
-        lat_spec = lat_transform(mode_data, cos_lat, sin_lat, False)
-        mixed_spec = block_mix(
-            lat_spec, first_all[layer_idx], bias_all[layer_idx], second_all[layer_idx], block_width
-        )
-        back_spec = lat_transform(mixed_spec, cos_lat, sin_lat, True).reshape(
-            ch_dev, lat_rows, 2 * per_piece
-        )
-        band_spec = lax.all_to_all(back_spec, "lat", split_axis=1, concat_axis=2, tiled=True)
-        spatial = jnp.dot(
-            band_spec.reshape(ch_dev * band_rows, lon_cells),
-            inverse,
-            preferred_element_type=jnp.float32,
-        )
-        spatial = spatial.reshape(ch_dev, band_rows, lon_cells)
-        summed = spatial + normed.astype(jnp.float32) + current.astype(jnp.float32)
+        normed_blocks = normed.reshape(block_count, block_width, band_rows, lon_cells)
+        received = []
+        for block in range(block_count):
+            lon_spec = jnp.dot(
+                normed_blocks[block].reshape(block_width * band_rows, lon_cells),
+                forward,
+                preferred_element_type=jnp.float32,
+            ).astype(jnp.bfloat16)
+            pieces = lon_spec.reshape(block_width, band_rows, lat_parts, 2 * per_piece)
+            pieces = pieces.transpose(2, 0, 1, 3)
+            received.append(exchange(pieces))
+        returned = []
+        for block in range(block_count):
+            mode_data = received[block].transpose(1, 0, 2, 3)
+            mode_data = mode_data.reshape(block_width, lat_rows, 2 * per_piece)
+            lat_spec = lat_transform(mode_data, cos_lat, sin_lat, False)
+            mixed_spec = block_mix(
+                lat_spec,
+                first_all[layer_idx][:, block : block + 1],
+                bias_all[layer_idx][:, block : block + 1],
+                second_all[layer_idx][:, block : block + 1],
+                block_width,
+            )
+            back_spec = lat_transform(mixed_spec, cos_lat, sin_lat, True)
+            pieces = back_spec.reshape(block_width, lat_parts, band_rows, 2 * per_piece)
+            returned.append(exchange(pieces.transpose(1, 0, 2, 3)))
+        current_blocks = current.reshape(block_count, block_width, band_rows, lon_cells)
+        summed_blocks = []
+        for block in range(block_count):
+            band_spec = returned[block].transpose(1, 2, 0, 3)
+            spatial = jnp.dot(
+                band_spec.reshape(block_width * band_rows, lon_cells),
+                inverse,
+                preferred_element_type=jnp.float32,
+            )
+            spatial = spatial.reshape(block_width, band_rows, lon_cells)
+            summed_blocks.append(
+                spatial
+                + normed_blocks[block].astype(jnp.float32)
+                + current_blocks[block].astype(jnp.float32)
+            )
+        summed = jnp.concatenate(summed_blocks, axis=0)
         energy = lax.psum(jnp.sum(area_weights * summed * summed), ("lat", "ch"))
         current = (summed * jnp.sqrt(target / energy)).astype(jnp.bfloat16)
         source = summed

time: 2740 us -> 2200 us (0.80)
  blocking collectives: 871 us -> 76 us
  local copies, waits for them, and re-layouts: 298 us -> 849 us
  waiting for transfers between devices: 844 us -> 466 us
  other arithmetic: 223 us -> 285 us
    all_to_all x1 -> x0, blocking collectives: 416 us -> none  [per_device(): lax.all_to_all(lon_spec.reshape(ch_dev, band_rows, lon_cells), 'lat', spl...]
    psum x1, blocking collectives: 416 us -> 38.1 us  [per_device(): target = lax.psum(jnp.sum(area_weights * source * source), ('lat', 'ch'))]
    all_to_all x3 -> x8, waiting for transfers between devices: 802 us -> 433 us  [exchange(): flat = lax.all_to_all(flat, 'lat', split_axis=0, concat_axis=0, tiled=True)]
    reshape x2 -> x24, local copies, waits for them, and re-layouts: 52.5 us -> 333 us  [the longest x8 124 us: exchange(): return lax.optimization_barrier(flat).reshape(parts, chans, rows, width_q)]
    slice x0 -> x20, local copies, waits for them, and re-layouts: none -> 190 us  [the longest x8 88.1 us: lat_transform(): real_part = part_cos[:, :, 0] - part_sin[:, :, 1]]
    unnamed x80 -> x118, local copies, waits for them, and re-layouts: 0.75 us -> 149 us
    dot_general x16 -> x32, matrix products: 186 us -> 62.7 us  [contract(): jnp.einsum('bcjm,bcd->bdjm', operand, weight, preferred_element_type=jnp....]
    all_to_all x4 -> x0, local copies, waits for them, and re-layouts: 114 us -> none  [the longest x2 72.2 us: per_device(): lax.all_to_all(lon_spec.reshape(ch_dev, band_rows, lon_cells), 'lat', spl...]
  transfers between devices with their start and end apart: 5 -> 10, of which waited for: 4 -> 7; matrix products, arithmetic and copies ran while one was open for 2% -> 39% of each run, Pallas kernels for 0% -> 0%
where the time goes in v1:
time: 2200 us; the launch traced here: 2180 us
  local copies, waits for them, and re-layouts  849 us (39%)
  waiting for transfers between devices  466 us (21%)
  matrix products  446 us (20%)
  other arithmetic  285 us (13%)
  blocking collectives  76 us (3%)
  starting transfers between devices  43.8 us (2%)
    all_to_all x8, waiting for transfers between devices, exchange(): flat = lax.all_to_all(flat, 'lat', split_axis=0, concat_axis=0, tiled=True)  433 us
    unnamed x118, local copies, waits for them, and re-layouts  149 us
    another operation x14, other arithmetic  146 us
    reshape x8, local copies, waits for them, and re-layouts, exchange(): return lax.optimization_barrier(flat).reshape(parts, chans, rows, width_q)  124 us
    reshape x8, local copies, waits for them, and re-layouts, exchange(): pieces.reshape(parts, chans, rows * width_q)  109 us
    dot_general x8, matrix products, lat_transform(): jnp.einsum('hj,chq->cjq', sin_lat, mode_data, preferred_element_type=jnp....  106 us
    dot_general x8, matrix products, lat_transform(): jnp.einsum('hj,chq->cjq', cos_lat, mode_data, preferred_element_type=jnp....  106 us
    reshape x8, local copies, waits for them, and re-layouts, per_device(): pieces = lon_spec.reshape(block_width, band_rows, lat_parts, 2 * per_piece)  99.9 us
  transfers between devices with their start and end apart: 10, of which 7 were waited for; matrix products, arithmetic and copies ran while one was open for 39% of the time, Pallas kernels for 0%

profile of v1, /device:TPU:0, one launch (start us, length us, event | category | flops | bytes accessed | tf_op | source)
XLA Modules:
  0.0 2183.3 jit_solution(12923259354208978704)
XLA Ops:
  28.6 32.9 %all-reduce.8.cloned.1.call-done = (bf16[48,768]{1,0:T(8,128)(2,1)}, bf16[48,768]{1,0:T(8,128)(2,1)}) async-done(((bf16[48,768]{1,0:T(8,128)(2,1)}, bf16[48,768]{1,0:T(8,128)(2,1)}), (bf16[48,768]{1,0:T(8,128)(2,1)}, bf16[48,768]{1,0:T(8,128)(2,1)})) %all-reduce.8.cloned.1.call-update) | async-done | bytes 147472 | tf_op jit(solution)/shard_map/psum | solution.py:41
  80.7 19.7 convolution_convert_fusion.3
  100.4 16.5 reshape.732
  125.4 15.7 reshape.733
  146.8 19.2 convolution_convert_fusion.2
  166.1 16.5 reshape.749
  191.1 15.7 reshape.750
  206.8 94.8 %all-to-all-done = bf16[8,96,4608]{2,1,0:T(8,128)(2,1)} async-done(((bf16[8,96,4608]{2,1,0:T(8,128)(2,1)}), bf16[8,96,4608]{2,1,0:T(8,128)(2,1)}, u32[]{:S(2)}, u32[]{:S(2)}) %all-to-all-start) | async-done | bytes 7077920 | tf_op jit(solution)/shard_map/all_to_all | solution.py:95
  309.2 15.5 reshape.734
  360.2 14.9 fusion.104
  386.0 18.1 fusion.48
  443.7 16.8 all-to-all-done.2
  460.5 15.3 reshape.751
  637.1 18.2 fusion.50
  702.5 14.9 fusion.26
  801.6 15.7 reshape.748
  817.3 18.2 copy.116
  835.5 15.3 dot_general.189
  850.8 104.3 %all-to-all-done.3 = bf16[8,96,4608]{2,1,0:T(8,128)(2,1)} async-done(((bf16[8,96,4608]{2,1,0:T(8,128)(2,1)}), bf16[8,96,4608]{2,1,0:T(8,128)(2,1)}, u32[]{:S(2)}, u32[]{:S(2)}) %all-to-all-start.3) | async-done | bytes 7077920 | tf_op jit(solution)/shard_map/all_to_all | solution.py:95
  955.1 15.4 reshape.765
  970.5 18.2 copy.132
  988.7 15.6 dot_general.204
  1004.4 23.9 %fusion.253 = (f32[48,768]{1,0:T(8,128)S(1)}, f32[96,48,768]{2,1,0:T(8,128)}) fusion(bf16[192,48,768]{2,1,0:T(8,128)(2,1)} %param.6, bf16[192,48,768]{2,1,0:T(8,128)(2,1)} %copy-done.4, bf16[96,48,768]{2,1,0:T(8,128)(2,1)} %dot_general.189, f32[768]{0:T(1024)S(1)} %compare_select_fusion, s32[768]{0:T(1024)S(1)} %copy-done.17, pred[768]{0:T(1024)(128)(4,1)S(1)} %copy-done.31), kind=kOutput, calls=%fused_computation.355 | convolution fusion | flops 5463502848 | bytes 35543808 | tf_op jit(solution)/shard_map/dot_general | solution.py:150
  1028.4 23.5 %fusion.254 = (f32[48,768]{1,0:T(8,128)S(1)}, f32[96,48,768]{2,1,0:T(8,128)}) fusion(bf16[192,48,768]{2,1,0:T(8,128)(2,1)S(1)} %bitcast.391, bf16[192,48,768]{2,1,0:T(8,128)(2,1)} %copy-done.4, bf16[96,48,768]{2,1,0:T(8,128)(2,1)} %dot_general.204, f32[768]{0:T(1024)S(1)} %compare_select_fusion, s32[768]{0:T(1024)S(1)} %copy-done.17, ...), kind=kOutput, calls=%fused_computation.356 | convolution fusion | flops 5463502848 | bytes 35543808 | tf_op jit(solution)/shard_map/dot_general | solution.py:150
  1066.1 38.1 %all-reduce = (f32[]{:T(128)}, f32[]{:T(128)}) all-reduce(f32[]{:T(128)} %get-tuple-element.7, f32[]{:T(128)} %get-tuple-element.5), channel_id=1, replica_groups=mesh['lat'=8,'ch'=4] {'lat','ch'}, use_global_device_ids=true, to_apply=%region_10.11 | all-reduce | flops 2 | bytes 16 | tf_op jit(solution)/shard_map/psum | solution.py:116
  1106.6 19.5 multiply_convert_fusion.1
  1134.2 19.6 convolution_convert_fusion.1
  1153.8 16.5 reshape.766
  1178.8 15.7 reshape.767
  1200.9 19.1 convolution_convert_fusion
  1219.9 16.5 reshape.783
  1244.9 15.7 reshape.784
  1260.6 94.0 %all-to-all-done.4 = bf16[8,96,4608]{2,1,0:T(8,128)(2,1)} async-done(((bf16[8,96,4608]{2,1,0:T(8,128)(2,1)}), bf16[8,96,4608]{2,1,0:T(8,128)(2,1)}, u32[]{:S(2)}, u32[]{:S(2)}) %all-to-all-start.4) | async-done | bytes 7077920 | tf_op jit(solution)/shard_map/all_to_all | solution.py:95
  1360.4 15.7 reshape.768
  1495.2 18.3 all-to-all-done.6
  1513.6 15.3 reshape.785
  1756.9 14.8 fusion.18
  1856.1 15.7 reshape.782
  1871.8 18.2 copy.150
  1890.0 15.3 dot_general.219
  1905.3 104.4 %all-to-all-done.7 = bf16[8,96,4608]{2,1,0:T(8,128)(2,1)} async-done(((bf16[8,96,4608]{2,1,0:T(8,128)(2,1)}), bf16[8,96,4608]{2,1,0:T(8,128)(2,1)}, u32[]{:S(2)}, u32[]{:S(2)}) %all-to-all-start.7) | async-done | bytes 7077920 | tf_op jit(solution)/shard_map/all_to_all | solution.py:95
  2009.7 15.4 reshape.799
  2025.1 18.2 copy.166
  2043.3 15.7 dot_general.234
  2059.0 23.5 %convert_add_fusion.1 = f32[96,48,768]{2,1,0:T(8,128)} fusion(bf16[96,48,768]{2,1,0:T(8,128)(2,1)} %dot_general.219, bf16[192,48,768]{2,1,0:T(8,128)(2,1)} %get-tuple-element.15, f32[768]{0:T(1024)S(1)} %copy-done.20, s32[768]{0:T(1024)S(1)} %copy-done.18, pred[768]{0:T(1024)(128)(4,1)S(1)} %copy-done.32, bf16[192,48,768]{2,1,0:T(8,128)(2,1)} %get-tuple-element.16), kind=kOutput, calls=%fused_computation.21 | convolution fusion | flops 5460000768 | bytes 35396352 | tf_op jit(solution)/shard_map/dot_general | solution.py:150
  2082.6 22.8 %convert_add_fusion = f32[96,48,768]{2,1,0:T(8,128)} fusion(bf16[96,48,768]{2,1,0:T(8,128)(2,1)} %dot_general.234, bf16[192,48,768]{2,1,0:T(8,128)(2,1)} %get-tuple-element.15, f32[768]{0:T(1024)S(1)} %copy-done.20, s32[768]{0:T(1024)S(1)} %copy-done.18, pred[768]{0:T(1024)(128)(4,1)S(1)} %copy-done.32, bf16[192,48,768]{2,1,0:T(8,128)(2,1)S(1)} %bitcast.409), kind=kOutput, calls=%fused_computation.20 | convolution fusion | flops 5460000768 | bytes 35396352 | tf_op jit(solution)/shard_map/dot_general | solution.py:150
  2118.8 37.9 %psum.55 = f32[]{:T(128)} all-reduce(f32[]{:T(128)} %fusion.1), channel_id=1, replica_groups=mesh['lat'=8,'ch'=4] {'lat','ch'}, use_global_device_ids=true, to_apply=%region_14.15 | all-reduce | flops 1 | bytes 8 | tf_op jit(solution)/shard_map/psum | solution.py:162
  2158.1 17.9 multiply_convert_fusion
  (256 shorter events, 947.0 us)
Async XLA Ops:
  6.5 54.9 %all-reduce.8.cloned.1.call-start = ((), (), s32[]{:S(2)}) async-start(), calls=%async_computation.9 | async-start | bytes 294912 | tf_op jit(solution)/shard_map/psum | solution.py:41
  14.2 13.3 copy-start.27
  14.2 13.8 copy-start.28
  27.5 119.3 %copy-start.16 = (s32[768]{0:T(1024)}, s32[768]{0:T(1024)S(1)}, u32[]{:S(2)}) copy-start(s32[768]{0:T(1024)S(1)} %fusion.129) | copy-start | bytes 9220
  28.6 118.2 %copy-start.30 = (pred[768]{0:T(1024)(128)(4,1)}, pred[768]{0:T(1024)(128)(4,1)S(1)}, u32[]{:S(2)}) copy-start(pred[768]{0:T(1024)(128)(4,1)S(1)} %fusion.131) | copy-start | bytes 2308
  141.1 160.5 %all-to-all-start = ((bf16[8,96,4608]{2,1,0:T(8,128)(2,1)}), bf16[8,96,4608]{2,1,0:T(8,128)(2,1)}, u32[]{:S(2)}, u32[]{:S(2)}) async-start(bf16[8,96,4608]{2,1,0:T(8,128)(2,1)} %reshape.733), calls=%async_computation | async-start | bytes 14155776 | tf_op jit(solution)/shard_map/all_to_all | solution.py:95
  206.8 99.7 %copy-start.9 = (bf16[2,2,2,96,96]{4,3,2,1,0:T(8,128)(2,1)S(1)}, bf16[2,2,2,96,96]{4,3,2,1,0:T(8,128)(2,1)}, u32[]{:S(2)}) copy-start(bf16[2,2,2,96,96]{4,3,2,1,0:T(8,128)(2,1)} %param.9) | copy-start | bytes 442372
  206.8 100.5 %copy-start.10 = (bf16[2,2,2,96,96]{4,3,2,1,0:T(8,128)(2,1)S(1)}, bf16[2,2,2,96,96]{4,3,2,1,0:T(8,128)(2,1)}, u32[]{:S(2)}) copy-start(bf16[2,2,2,96,96]{4,3,2,1,0:T(8,128)(2,1)} %param.11) | copy-start | bytes 442372
  206.8 101.3 %copy-start.29 = (bf16[2,2,2,96]{3,2,1,0:T(2,128)(2,1)S(1)}, bf16[2,2,2,96]{3,2,1,0:T(2,128)(2,1)}, u32[]{:S(2)}) copy-start(bf16[2,2,2,96]{3,2,1,0:T(2,128)(2,1)} %param.10) | copy-start | bytes 4612
  301.6 158.9 %all-to-all-start.2 = ((bf16[8,96,4608]{2,1,0:T(8,128)(2,1)}), bf16[8,96,4608]{2,1,0:T(8,128)(2,1)}, u32[]{:S(2)}, u32[]{:S(2)}) async-start(bf16[8,96,4608]{2,1,0:T(8,128)(2,1)} %reshape.750), calls=%async_computation.2 | async-start | bytes 14155776 | tf_op jit(solution)/shard_map/all_to_all | solution.py:95
  308.1 102.7 %copy-start.5 = (bf16[1,2,2,96,96]{3,4,2,1,0:T(8,128)(2,1)}, bf16[1,2,2,96,96]{3,4,2,1,0:T(8,128)(2,1)S(1)}, u32[]{:S(2)}) copy-start(bf16[1,2,2,96,96]{3,4,2,1,0:T(8,128)(2,1)S(1)} %copy.181) | copy-start | bytes 221188
  485.8 14.6 copy-start
  610.1 185.4 %all-to-all-start.1 = ((bf16[8,96,4608]{2,1,0:T(8,128)(2,1)}), bf16[8,96,4608]{2,1,0:T(8,128)(2,1)}, u32[]{:S(2)}, u32[]{:S(2)}) async-start(bf16[8,96,4608]{2,1,0:T(8,128)(2,1)} %copy.175), calls=%async_computation.1 | async-start | bytes 14155776 | tf_op jit(solution)/shard_map/all_to_all | solution.py:95
  670.3 12.0 copy-start.2
  795.5 159.6 %all-to-all-start.3 = ((bf16[8,96,4608]{2,1,0:T(8,128)(2,1)}), bf16[8,96,4608]{2,1,0:T(8,128)(2,1)}, u32[]{:S(2)}, u32[]{:S(2)}) async-start(bf16[8,96,4608]{2,1,0:T(8,128)(2,1)} %copy.176), calls=%async_computation.3 | async-start | bytes 14155776 | tf_op jit(solution)/shard_map/all_to_all | solution.py:95
  801.5 304.1 %all-reduce.6.cloned.1.call-start = ((), (), s32[]{:S(2)}) async-start(), calls=%async_computation.8 | async-start | bytes 294912 | tf_op jit(solution)/shard_map/psum | solution.py:41
  801.6 226.7 %copy-start.19 = (f32[768]{0:T(1024)}, f32[768]{0:T(1024)S(1)}, u32[]{:S(2)}) copy-start(f32[768]{0:T(1024)S(1)} %compare_select_fusion) | copy-start | bytes 9220
  988.7 15.6 copy-start.17
  988.7 15.6 copy-start.31
  988.7 39.6 %slice-start = ((s8[14155776]{0:T(1024)(128)(4,1)}), s8[1572864]{0:T(1024)(128)(4,1)S(1)}, s32[]{:S(2)}) async-start(s8[14155776]{0:T(1024)(128)(4,1)} %bitcast.390), calls=%async_computation.10 | async-start | bytes 3145728
  1004.4 24.0 %slice-start.1 = ((s8[14155776]{0:T(1024)(128)(4,1)}), s8[4194304]{0:T(1024)(128)(4,1)S(1)}, s32[]{:S(2)}) async-start(s8[14155776]{0:T(1024)(128)(4,1)} %bitcast.390), calls=%async_computation.11 | async-start | bytes 8388608
  1004.4 24.0 %slice-start.2 = ((s8[14155776]{0:T(1024)(128)(4,1)}), s8[4194304]{0:T(1024)(128)(4,1)S(1)}, s32[]{:S(2)}) async-start(s8[14155776]{0:T(1024)(128)(4,1)} %bitcast.390), calls=%async_computation.12 | async-start | bytes 8388608
  1004.4 24.0 %slice-start.3 = ((s8[14155776]{0:T(1024)(128)(4,1)}), s8[4194304]{0:T(1024)(128)(4,1)S(1)}, s32[]{:S(2)}) async-start(s8[14155776]{0:T(1024)(128)(4,1)} %bitcast.390), calls=%async_computation.13 | async-start | bytes 8388608
  1028.4 24.2 %copy-start.12 = (f32[48]{0:T(128)S(1)}, f32[48]{0:T(128)}, u32[]{:S(2)}) copy-start(f32[48]{0:T(128)} %copy-done.11) | copy-start | bytes 580
  1052.5 54.0 %copy-start.14 = (f32[1,192]{1,0:T(1,128)S(1)}, f32[1,192]{1,0:T(1,128)}, u32[]{:S(2)}) copy-start(f32[1,192]{1,0:T(1,128)} %get-tuple-element.64) | copy-start | bytes 2308
  1052.5 54.0 %copy-start.15 = (f32[1,192]{1,0:T(1,128)S(1)}, f32[1,192]{1,0:T(1,128)}, u32[]{:S(2)}) copy-start(f32[1,192]{1,0:T(1,128)} %get-tuple-element.66) | copy-start | bytes 2308
  1194.5 160.2 %all-to-all-start.4 = ((bf16[8,96,4608]{2,1,0:T(8,128)(2,1)}), bf16[8,96,4608]{2,1,0:T(8,128)(2,1)}, u32[]{:S(2)}, u32[]{:S(2)}) async-start(bf16[8,96,4608]{2,1,0:T(8,128)(2,1)} %reshape.767), calls=%async_computation.4 | async-start | bytes 14155776 | tf_op jit(solution)/shard_map/all_to_all | solution.py:95
  1260.6 98.9 %copy-start.7 = (bf16[1,2,2,96,96]{4,3,2,1,0:T(8,128)(2,1)S(1)}, bf16[1,2,2,96,96]{4,3,2,1,0:T(8,128)(2,1)}, u32[]{:S(2)}) copy-start(bf16[1,2,2,96,96]{4,3,2,1,0:T(8,128)(2,1)} %get-tuple-element.55) | copy-start | bytes 221188
  1260.6 99.0 %copy-start.8 = (bf16[1,2,2,96,96]{4,3,2,1,0:T(8,128)(2,1)S(1)}, bf16[1,2,2,96,96]{4,3,2,1,0:T(8,128)(2,1)}, u32[]{:S(2)}) copy-start(bf16[1,2,2,96,96]{4,3,2,1,0:T(8,128)(2,1)} %get-tuple-element.53) | copy-start | bytes 221188
  1260.6 99.2 %copy-start.22 = (f32[2,1,96]{2,1,0:T(1,128)S(1)}, f32[2,1,96]{2,1,0:T(1,128)}, u32[]{:S(2)}) copy-start(f32[2,1,96]{2,1,0:T(1,128)} %get-tuple-element.69) | copy-start | bytes 2308
  1260.6 99.2 %copy-start.21 = (f32[2,1,96]{2,1,0:T(1,128)S(1)}, f32[2,1,96]{2,1,0:T(1,128)}, u32[]{:S(2)}) copy-start(f32[2,1,96]{2,1,0:T(1,128)} %get-tuple-element.70) | copy-start | bytes 2308
  1354.7 158.9 %all-to-all-start.6 = ((bf16[8,96,4608]{2,1,0:T(8,128)(2,1)}), bf16[8,96,4608]{2,1,0:T(8,128)(2,1)}, u32[]{:S(2)}, u32[]{:S(2)}) async-start(bf16[8,96,4608]{2,1,0:T(8,128)(2,1)} %reshape.784), calls=%async_computation.6 | async-start | bytes 14155776 | tf_op jit(solution)/shard_map/all_to_all | solution.py:95
  1426.1 24.1 %slice-start.8 = ((s8[7077888]{0:T(1024)(128)(4,1)}), s8[2883584]{0:T(1024)(128)(4,1)S(1)}, s32[]{:S(2)}) async-start(s8[7077888]{0:T(1024)(128)(4,1)} %bitcast.434), calls=%async_computation.18 | async-start | bytes 5767168
  1437.2 13.0 slice-start.9
  1539.0 14.7 copy-start.1
  1663.5 186.7 %all-to-all-start.5 = ((bf16[8,96,4608]{2,1,0:T(8,128)(2,1)}), bf16[8,96,4608]{2,1,0:T(8,128)(2,1)}, u32[]{:S(2)}, u32[]{:S(2)}) async-start(bf16[8,96,4608]{2,1,0:T(8,128)(2,1)} %copy.177), calls=%async_computation.5 | async-start | bytes 14155776 | tf_op jit(solution)/shard_map/all_to_all | solution.py:95
  1679.5 24.1 %slice-start.10 = ((s8[7077888]{0:T(1024)(128)(4,1)}), s8[2883584]{0:T(1024)(128)(4,1)S(1)}, s32[]{:S(2)}) async-start(s8[7077888]{0:T(1024)(128)(4,1)} %bitcast.436), calls=%async_computation.20 | async-start | bytes 5767168
  1690.6 13.0 slice-start.11
  1724.3 12.3 copy-start.3
  1850.2 159.4 %all-to-all-start.7 = ((bf16[8,96,4608]{2,1,0:T(8,128)(2,1)}), bf16[8,96,4608]{2,1,0:T(8,128)(2,1)}, u32[]{:S(2)}, u32[]{:S(2)}) async-start(bf16[8,96,4608]{2,1,0:T(8,128)(2,1)} %copy.178), calls=%async_computation.7 | async-start | bytes 14155776 | tf_op jit(solution)/shard_map/all_to_all | solution.py:95
  2043.3 15.7 copy-start.18
  2043.3 15.7 copy-start.20
  2043.3 15.7 copy-start.32
  2043.3 39.3 %slice-start.4 = ((s8[14155776]{0:T(1024)(128)(4,1)}), s8[1572864]{0:T(1024)(128)(4,1)S(1)}, s32[]{:S(2)}) async-start(s8[14155776]{0:T(1024)(128)(4,1)} %bitcast.408), calls=%async_computation.14 | async-start | bytes 3145728
  2059.0 23.6 %slice-start.5 = ((s8[14155776]{0:T(1024)(128)(4,1)}), s8[4194304]{0:T(1024)(128)(4,1)S(1)}, s32[]{:S(2)}) async-start(s8[14155776]{0:T(1024)(128)(4,1)} %bitcast.408), calls=%async_computation.15 | async-start | bytes 8388608
  2059.0 23.6 %slice-start.6 = ((s8[14155776]{0:T(1024)(128)(4,1)}), s8[4194304]{0:T(1024)(128)(4,1)S(1)}, s32[]{:S(2)}) async-start(s8[14155776]{0:T(1024)(128)(4,1)} %bitcast.408), calls=%async_computation.16 | async-start | bytes 8388608
  2059.0 23.6 %slice-start.7 = ((s8[14155776]{0:T(1024)(128)(4,1)}), s8[4194304]{0:T(1024)(128)(4,1)S(1)}, s32[]{:S(2)}) async-start(s8[14155776]{0:T(1024)(128)(4,1)} %bitcast.408), calls=%async_computation.17 | async-start | bytes 8388608
  2082.6 22.8 %copy-start.13 = (f32[48]{0:T(128)S(1)}, f32[48]{0:T(128)}, u32[]{:S(2)}) copy-start(f32[48]{0:T(128)} %copy-done.11) | copy-start | bytes 580
  (11 other events, 32.1 us)
Sparse Core Ops, SparseCore 0:
  27.6 33.8 all-reduce.7
  1066.2 29.7 all-reduce.5
